TPU v7x, 32 devices: a whole 2x2x4 slice. The times are simulated.
32 devices in a mesh: seq: 8 (over y, x, core), tp: 4 (over z).
Axes of the slice: x: 2, y: 2, z: 4, core: 2. Of those that a mesh axis runs over, the one named last changes fastest.
Arguments:
- hidden: bfloat16 [8192, 2560], P('seq', 'tp'), may hold values from -6 to 6
- gate_proj: bfloat16 [2560, 5120], P(None, 'tp'), may hold values from -0.125 to 0.125
- input_proj: bfloat16 [2560, 5120], P(None, 'tp'), may hold values from -0.125 to 0.125
- bc_proj: bfloat16 [2560, 256], replicated, may hold values from -0.125 to 0.125
- step_proj: bfloat16 [2560, 80], P(None, 'tp'), may hold values from -0.125 to 0.125
- step_bias: float32 [80], P('tp'), may hold values from -16 to -3
- decay_log: float32 [80], P('tp'), may hold values from 0 to 2.78
- conv_weight: float32 [4, 5120], P(None, 'tp'), may hold values from -3 to 3
- conv_bias: float32 [5120], P('tp'), may hold values from -3 to 3
- bc_conv_weight: float32 [4, 256], replicated, may hold values from -3 to 3
- bc_conv_bias: float32 [256], replicated, may hold values from -3 to 3
- skip_gain: float32 [80], P('tp'), may hold values from 0.5 to 2
- norm_gain: float32 [5120], P('tp'), may hold values from 0.1 to 1.9
- out_proj: bfloat16 [5120, 2560], P('tp'), may hold values from -0.078125 to 0.078125
- amax_history: float32 [16], replicated, may hold values from 1.5 to 4
Outputs:
- mixed: bfloat16 [8192, 2560], P('seq', 'tp')
- new_history: float32 [16], replicated
All inputs are finite; a program needn't handle non-finite values.
Results may differ from a plain program's by a relative error of at most 0.015.
Values may be sent and summed in bfloat16 or wider, within the bound.
A program may use at most 192 MiB of HBM per device.

v0:
```python
import jax
import jax.numpy as jnp
from jax import lax
from jax.sharding import PartitionSpec as P

BLOCK = 256
INNER = 5120
QMAX = 448.0
EPS = 1e-05


def shifted(x, axis, by):
    size = lax.axis_size(axis)
    pairs = [(i, i + by) for i in range(size) if 0 <= i + by < size]
    return lax.ppermute(x, axis, pairs)


def carried_in(x, axis, join, neutral):
    place = lax.axis_index(axis)
    gathered = jax.tree.map(
        lambda a, kind: lax.all_gather(a.astype(kind), axis), x, (jnp.bfloat16, jnp.bfloat16)
    )
    state = jax.tree.map(lambda a, e: jnp.zeros_like(a) + jnp.asarray(e, a.dtype), x, neutral)

    def one(turn, state):
        return join(
            state,
            jax.tree.map(
                lambda a, own: lax.dynamic_index_in_dim(a, turn, 0, False).astype(own.dtype),
                gathered,
                x,
            ),
        )

    return lax.fori_loop(0, place, one, state)


def conv_silu(pre_conv, rim_rows, weight, conv_shift):
    row_count = pre_conv.shape[0]
    kernel = weight.shape[0]
    padded = jnp.concatenate([rim_rows, pre_conv], axis=0)
    running = jnp.zeros(pre_conv.shape, jnp.float32)
    for offset in range(kernel):
        running = running + weight[offset] * padded[offset : offset + row_count].astype(jnp.float32)
    return jax.nn.silu(running + conv_shift).astype(jnp.bfloat16)


def ssd_block(carry_state, block_data):
    x_block, b_block, c_block, step_block, decay_block = block_data
    length = x_block.shape[0]
    head_count = carry_state.shape[0]
    head_width = carry_state.shape[1]
    cum_decay = jnp.cumsum(decay_block, axis=1)
    scores = jnp.dot(c_block, b_block.T, preferred_element_type=jnp.float32)
    causal = lax.broadcasted_iota(jnp.int32, (length, length), 0) >= lax.broadcasted_iota(
        jnp.int32, (length, length), 1
    )
    decay_gap = cum_decay[:, :, None] - cum_decay[:, None, :]
    decay_mask = jnp.where(causal, jnp.exp(jnp.where(causal, decay_gap, 0.0)), 0.0)
    weights = (scores[None] * decay_mask * step_block[:, None, :]).astype(jnp.bfloat16)
    x_heads = x_block.reshape(length, head_count, head_width)
    intra_out = jnp.einsum("hts,shp->htp", weights, x_heads, preferred_element_type=jnp.float32)
    inter_out = jnp.exp(cum_decay)[:, :, None] * jnp.einsum(
        "tn,hpn->htp", c_block.astype(jnp.float32), carry_state, precision=lax.Precision.HIGHEST
    )
    tail_decay = jnp.exp(cum_decay[:, -1:] - cum_decay) * step_block
    x_weighted = (tail_decay.T[:, :, None] * x_heads.astype(jnp.float32)).astype(jnp.bfloat16)
    update = jnp.einsum("shp,sn->hpn", x_weighted, b_block, preferred_element_type=jnp.float32)
    next_state = jnp.exp(cum_decay[:, -1])[:, None, None] * carry_state + update
    block_out = (intra_out + inter_out).transpose(1, 0, 2).reshape(length, head_count * head_width)
    return (next_state, block_out)


def chain(earlier, later):
    return (earlier[0] + later[0], jnp.exp(later[0])[..., None, None] * earlier[1] + later[1])


def shards(
    hidden,
    gate_proj,
    input_proj,
    bc_proj,
    step_proj,
    step_bias,
    decay_log,
    conv_weight,
    conv_bias,
    bc_conv_weight,
    bc_conv_bias,
    skip_gain,
    norm_gain,
    out_proj,
    amax_history,
):
    row_count = hidden.shape[0]
    inner_local = gate_proj.shape[1]
    state_width = bc_proj.shape[1] // 2
    head_count = step_proj.shape[1]
    head_width = inner_local // head_count
    kernel = conv_weight.shape[0]
    matrices = (gate_proj, input_proj, bc_proj, step_proj)
    piece = lax.all_gather(hidden, "tp", axis=1, tiled=True)
    gate_raw, x_raw, bc_raw, step_raw = tuple(
        (jnp.dot(piece, matrix, preferred_element_type=jnp.float32) for matrix in matrices)
    )
    gate_in = gate_raw.astype(jnp.bfloat16)
    x_pre = x_raw.astype(jnp.bfloat16)
    bc_pre = bc_raw.astype(jnp.bfloat16)
    x_rim, bc_rim = shifted(
        (x_pre[row_count - kernel + 1 :], bc_pre[row_count - kernel + 1 :]), "seq", 1
    )
    x_conv = conv_silu(x_pre, x_rim, conv_weight, conv_bias)
    bc_conv = conv_silu(bc_pre, bc_rim, bc_conv_weight, bc_conv_bias)
    b_in = bc_conv[:, :state_width]
    c_out = bc_conv[:, state_width:]
    step_size = jax.nn.softplus(step_raw + step_bias)
    log_decay = step_size * -jnp.exp(decay_log)
    blocks = row_count // BLOCK
    stacked = (
        x_conv.reshape(blocks, BLOCK, inner_local),
        b_in.reshape(blocks, BLOCK, state_width),
        c_out.reshape(blocks, BLOCK, state_width),
        step_size.reshape(blocks, BLOCK, head_count).transpose(0, 2, 1),
        log_decay.reshape(blocks, BLOCK, head_count).transpose(0, 2, 1),
    )
    zero_state = jnp.zeros((head_count, head_width, state_width), jnp.float32)
    local_state, block_outs = lax.scan(ssd_block, zero_state, stacked)
    total_decay = jnp.sum(log_decay, axis=0)
    entry_decay, incoming = carried_in(
        (total_decay, local_state), "seq", chain, (jnp.zeros_like(total_decay), zero_state)
    )
    reach = jnp.exp(jnp.cumsum(log_decay, axis=0))
    carried = jnp.einsum(
        "tn,hpn->thp", c_out.astype(jnp.float32), incoming, precision=lax.Precision.HIGHEST
    )
    ssm_out = block_outs.reshape(row_count, inner_local) + (reach[:, :, None] * carried).reshape(
        row_count, inner_local
    )
    x_heads = x_conv.reshape(row_count, head_count, head_width).astype(jnp.float32)
    ssm_out = ssm_out + (skip_gain[:, None] * x_heads).reshape(row_count, inner_local)
    gated = ssm_out * jax.nn.silu(gate_in.astype(jnp.float32))
    local_squares = jnp.sum(gated * gated, axis=1)
    squares = lax.psum(local_squares, "tp")
    inv_rms = lax.rsqrt(squares / INNER + EPS)
    normed = gated * inv_rms[:, None] * norm_gain
    peak_value = lax.pmax(jnp.max(jnp.abs(normed)), ("seq", "tp"))
    scale = QMAX / jnp.max(amax_history)
    quant = jnp.clip(normed * scale, -QMAX, QMAX).astype(jnp.bfloat16)
    partial_value = jnp.dot(quant, out_proj, preferred_element_type=jnp.float32)
    summed = lax.psum_scatter(
        partial_value.astype(jnp.bfloat16), "tp", scatter_dimension=1, tiled=True
    ).astype(jnp.float32)
    mixed = (summed / scale).astype(jnp.bfloat16)
    new_history = jnp.concatenate([jnp.reshape(peak_value, (1,)), amax_history[:-1]])
    return (mixed, new_history)


def solution(mesh):
    return jax.shard_map(
        shards,
        mesh=mesh,
        in_specs=(
            P("seq", "tp"),
            P(None, "tp"),
            P(None, "tp"),
            P(),
            P(None, "tp"),
            P("tp"),
            P("tp"),
            P(None, "tp"),
            P("tp"),
            P(),
            P(),
            P("tp"),
            P("tp"),
            P("tp", None),
            P(),
        ),
        out_specs=(P("seq", "tp"), P()),
        check_vma=False,
    )
```

profile of v0, /device:TPU:0, one launch (start us, length us, event | category | flops | bytes accessed | tf_op | source)
XLA Modules:
  0.0 387.2 jit_solution(16911178018496801252)
XLA Ops:
  10.4 100.0 %all-gather.5.cloned.1.call-done = bf16[1024,2560]{1,0:T(8,128)(2,1)} async-done(((bf16[1024,640]{1,0:T(8,128)(2,1)}), bf16[1024,2560]{1,0:T(8,128)(2,1)}) %all-gather.5.cloned.1.call-update) | async-done | bytes 5242896 | tf_op jit(solution)/shard_map/all_gather | solution.py:102
  110.4 4.1 %convolution_convert_fusion.3 = bf16[1024,256]{1,0:T(8,128)(2,1)S(1)} fusion(bf16[1024,2560]{1,0:T(8,128)(2,1)} %all-gather.5.cloned.1.call-done, bf16[2560,256]{1,0:T(8,128)(2,1)S(1)} %copy-done), kind=kOutput, calls=%fused_computation.71 | convolution fusion | flops 1342439424 | bytes 7077888 | tf_op jit(solution)/shard_map/dot_general | solution.py:104
  114.6 1.9 collective-permute-start.1
  116.5 10.0 %convolution_convert_fusion.2 = bf16[1024,1280]{1,0:T(8,128)(2,1)S(1)} fusion(bf16[1024,2560]{1,0:T(8,128)(2,1)S(1)} %copy-done.3, bf16[2560,1280]{1,0:T(8,128)(2,1)} %param.21), kind=kOutput, calls=%fused_computation.58 | convolution fusion | flops 6712197120 | bytes 14417920 | tf_op jit(solution)/shard_map/dot_general | solution.py:104
  126.5 3.8 collective-permute-start
  130.3 2.2 fusion.42
  134.3 8.2 %multiply_convert_fusion.4 = bf16[1024,1280]{1,0:T(8,128)(2,1)} fusion(bf16[1024,1280]{1,0:T(8,128)(2,1)} %copy-done.8, bf16[3,1280]{1,0:T(4,128)(2,1)S(1)} %collective-permute-done, f32[1280]{0:T(1024)S(1)} %copy-done.10, f32[1280]{0:T(1024)S(1)} %get-tuple-element.153, f32[1280]{0:T(1024)S(1)} %get-tuple-element.154, f32[1280]{0:T(1024)S(1)} %get-tuple-element.152, ...), kind=kLoop, calls=%fused_computation.56 | loop fusion | flops 34078720 | bytes 5276160 | tf_op jit(solution)/shard_map/convert_element_type | solution.py:45
  142.5 48.7 %while.26 = (s32[]{:T(128)}, f32[20,64,128]{2,1,0:T(8,128)S(1)}, f32[4,256,1280]{2,1,0:T(8,128)}, f32[4,20,256]{2,1,0:T(8,128)}, f32[4,20,256]{2,1,0:T(8,128)}, ...) while((s32[]{:T(128)}, f32[20,64,128]{2,1,0:T(8,128)S(1)}, ...), condition=%wide.region_3.4_spmd.clone, body=%wide.region_0.3_spmd.clone.sunk | while | flops 782641216 | bytes 22548344 | solution.py:127
  144.5 1.4 multiply_bitcast_fusion.2
  147.5 1.7 fusion.85
  149.2 1.4 fusion.86
  151.1 1.2 constant_dynamic-update-slice_fusion.2
  152.3 1.2 fusion.83
  153.5 1.2 convolution_add_fusion.3
  156.7 1.4 multiply_bitcast_fusion.2
  159.7 1.7 fusion.85
  161.4 1.4 fusion.86
  163.3 1.1 constant_dynamic-update-slice_fusion.2
  164.4 1.2 fusion.83
  165.6 1.2 convolution_add_fusion.3
  168.8 1.4 multiply_bitcast_fusion.2
  171.8 1.7 fusion.85
  173.5 1.4 fusion.86
  175.4 1.3 constant_dynamic-update-slice_fusion.2
  176.6 1.2 fusion.83
  177.9 1.2 convolution_add_fusion.3
  181.0 1.4 multiply_bitcast_fusion.2
  184.1 1.7 fusion.85
  185.8 1.4 fusion.86
  187.6 1.2 constant_dynamic-update-slice_fusion.2
  188.8 1.2 fusion.83
  190.0 1.2 convolution_add_fusion.3
  192.4 1.2 dynamic-slice
  195.8 12.1 %all-reduce = bf16[160]{0:T(256)(128)(2,1)S(1)} all-reduce(bf16[160]{0:T(256)(128)(2,1)S(1)} %dynamic-update-slice), channel_id=2, replica_groups=mesh['seq'=8,'tp'=4] {'seq'}, use_global_device_ids=true, to_apply=%add | all-reduce | flops 160 | bytes 640
  208.9 5.6 %reduce-window.16 = f32[20,8,128]{2,1,0:T(8,128)S(1)} reduce-window(f32[20,8,128]{2,1,0:T(8,128)S(1)} %slice.113, f32[]{:T(128)} %constant.62.clone.1), window={size=1x1x128 pad=0_0x0_0x127_0}, to_apply=%region_4.5 | reduce-window | flops 2600960 | bytes 163844 | tf_op jit(solution)/shard_map/reduce-window.2
  215.0 4.7 %all-gather.7.cloned.1.call-done = bf16[160,64,128]{2,1,0:T(8,128)(2,1)} async-done(((bf16[20,64,128]{2,1,0:T(8,128)(2,1)}), bf16[160,64,128]{2,1,0:T(8,128)(2,1)}) %all-gather.7.cloned.1.call-update) | async-done | bytes 2621456 | tf_op jit(solution)/shard_map/all_gather | solution.py:21
  219.8 4.6 %broadcast_multiply_fusion = f32[1024,20,64]{0,2,1:T(8,128)} fusion(f32[1024,20]{0,1:T(8,128)S(1)} %bitcast.151, f32[20,64,128]{2,1,0:T(8,128)S(1)} %get-tuple-element.91, bf16[1024,256]{1,0:T(8,128)(2,1)S(1)} %copy-done.5), kind=kOutput, calls=%fused_computation.69 | convolution fusion | flops 2014576640 | bytes 6258688 | tf_op jit(solution)/shard_map/tn,hpn->thp/dot_general | solution.py:133
  224.4 5.9 %copy.53 = f32[1024,1280]{1,0:T(8,128)} copy(f32[1024,1280]{0,1:T(8,128)} %bitcast.139) | data formatting | bytes 10485760 | tf_op jit(solution)/shard_map/reshape | solution.py:136
  230.2 15.6 %multiply_reduce_fusion = (f32[1024]{0:T(1024)S(1)}, f32[1024,1280]{1,0:T(8,128)}) fusion(bf16[1024,2560]{1,0:T(8,128)(2,1)} %all-gather.5.cloned.1.call-done, bf16[2560,1280]{1,0:T(8,128)(2,1)} %param.20, bf16[1024,1280]{1,0:T(8,128)(2,1)} %bitcast.142, f32[1280]{0:T(1024)S(1)} %mul.247, f32[1024,1280]{1,0:T(8,128)} %copy.53, ...), kind=kOutput, calls=%fused_computation.55 | convolution fusion | flops 6727924736 | bytes 30155776 | tf_op jit(solution)/shard_map/dot_general | solution.py:104
  245.8 11.7 %psum.7 = f32[1024]{0:T(1024)S(1)} all-reduce(f32[1024]{0:T(1024)S(1)} %get-tuple-element.195), channel_id=1, replica_groups=mesh['seq'=8,'tp'=4] {'tp'}, use_global_device_ids=true, to_apply=%region_10.11 | all-reduce | flops 1024 | bytes 8192 | tf_op jit(solution)/shard_map/psum | solution.py:143
  257.5 12.8 %convolution_convert_fusion = bf16[1024,2560]{1,0:T(8,128)(2,1)} fusion(bf16[1280,2560]{1,0:T(8,128)(2,1)} %param.32, f32[1024,1280]{1,0:T(8,128)} %get-tuple-element.196, f32[]{:T(128)S(6)} %div.31, f32[1280]{0:T(1024)S(1)} %copy-done.11, f32[1024]{0:T(1024)S(1)} %add_rsqrt_fusion), kind=kOutput, calls=%fused_computation.45 | convolution fusion | flops 6720061440 | bytes 17048580 | tf_op jit(solution)/shard_map/dot_general | solution.py:149
  270.3 8.0 %copy.54 = bf16[1024,2560]{0,1:T(8,128)(2,1)} copy(bf16[1024,2560]{1,0:T(8,128)(2,1)} %convolution_convert_fusion) | data formatting | bytes 10485760
  278.3 4.0 %abs_reduce_fusion = f32[]{:T(128)} fusion(f32[1024,1280]{1,0:T(8,128)} %get-tuple-element.196, f32[1280]{0:T(1024)S(1)} %copy-done.11, f32[1024]{0:T(1024)S(1)} %add_rsqrt_fusion), kind=kLoop, calls=%fused_computation.52 | loop fusion | flops 5242879 | bytes 5252100 | tf_op jit(solution)/shard_map/reduce_max | solution.py:146
  282.2 51.0 %pmax.7 = f32[1]{0:T(128)} all-reduce(f32[1]{0:T(128)} %bitcast.19), channel_id=1, replica_groups=mesh['seq'=8,'tp'=4] {'seq','tp'}, use_global_device_ids=true, to_apply=%region_14.15 | all-reduce | flops 1 | bytes 8 | tf_op jit(solution)/shard_map/pmax | solution.py:146
  333.2 1.2 pad_maximum_fusion.2
  334.5 43.2 %reduce-scatter.4.cloned.1.call-done = bf16[640,1024]{1,0:T(8,128)(2,1)} async-done(((bf16[2560,1024]{1,0:T(8,128)(2,1)}), bf16[640,1024]{1,0:T(8,128)(2,1)}) %reduce-scatter.4.cloned.1.call-update) | async-done | bytes 1310736
  377.7 1.7 copy.55
  379.4 1.3 divide_convert_fusion
  (163 shorter events, 24.2 us)
Async XLA Ops:
  7.2 103.2 %copy-start = (bf16[2560,256]{1,0:T(8,128)(2,1)S(1)}, bf16[2560,256]{1,0:T(8,128)(2,1)}, u32[]{:S(2)}) copy-start(bf16[2560,256]{1,0:T(8,128)(2,1)} %param.22) | copy-start | bytes 3932164
  7.2 103.2 %all-gather.5.cloned.1.call-start = ((), (), s32[]{:S(2)}) async-start(), calls=%async_computation.1 | async-start | bytes 6553600 | tf_op jit(solution)/shard_map/all_gather | solution.py:102
  7.9 211.8 %all-gather.7.cloned.1.call-start = ((), (), s32[]{:S(2)}) async-start(), calls=%async_computation.2 | async-start | bytes 2949120 | tf_op jit(solution)/shard_map/all_gather | solution.py:21
  110.4 6.1 %copy-start.3 = (bf16[1024,2560]{1,0:T(8,128)(2,1)S(1)}, bf16[1024,2560]{1,0:T(8,128)(2,1)}, u32[]{:S(2)}) copy-start(bf16[1024,2560]{1,0:T(8,128)(2,1)} %all-gather.5.cloned.1.call-done) | copy-start | bytes 15728644
  114.6 15.8 %copy-start.9 = (bf16[2560,20]{0,1:T(8,128)(2,1)S(1)}, bf16[2560,20]{0,1:T(8,128)(2,1)}, u32[]{:S(2)}) copy-start(bf16[2560,20]{0,1:T(8,128)(2,1)} %param.23) | copy-start | bytes 307204
  114.6 15.8 %copy-start.12 = (f32[20]{0:T(128)S(1)}, f32[20]{0:T(128)}, u32[]{:S(2)}) copy-start(f32[20]{0:T(128)} %param.24) | copy-start | bytes 244
  114.6 18.9 %collective-permute-start.1 = (bf16[3,256]{1,0:T(4,128)(2,1)S(1)}, bf16[3,256]{1,0:T(4,128)(2,1)S(1)}, u32[]{:S(2)}, u32[]{:S(2)}) collective-permute-start(bf16[3,256]{1,0:T(4,128)(2,1)S(1)} %slice.104), channel_id=1, source_target_pairs={{0,4},{4,8},{8,12},{12,16},{16,20},{20,24},{24,28},{1,5},{5,9},{9,... | collective-permute-start | bytes 4616 | tf_op jit(solution)/shard_map/ppermute | solution.py:15
  126.5 6.0 %copy-start.8 = (bf16[1024,1280]{1,0:T(8,128)(2,1)}, bf16[1024,1280]{1,0:T(8,128)(2,1)S(1)}, u32[]{:S(2)}) copy-start(bf16[1024,1280]{1,0:T(8,128)(2,1)S(1)} %convolution_convert_fusion.2) | copy-start | bytes 7864324
  126.5 7.0 %copy-start.13 = (f32[256]{0:T(256)S(1)}, f32[256]{0:T(256)}, u32[]{:S(2)}) copy-start(f32[256]{0:T(256)} %param.29) | copy-start | bytes 3076
  126.5 7.8 %copy-start.10 = (f32[1280]{0:T(1024)S(1)}, f32[1280]{0:T(1024)}, u32[]{:S(2)}) copy-start(f32[1280]{0:T(1024)} %param.27) | copy-start | bytes 15364
  126.5 7.7 %collective-permute-start = (bf16[3,1280]{1,0:T(4,128)(2,1)S(1)}, bf16[3,1280]{1,0:T(4,128)(2,1)S(1)}, u32[]{:S(2)}, u32[]{:S(2)}) collective-permute-start(bf16[3,1280]{1,0:T(4,128)(2,1)S(1)} %slice.99), channel_id=1, source_target_pairs={{0,4},{4,8},{8,12},{12,16},{16,20},{20,24},{24,28},{1,5},{5,9},{9,... | collective-permute-start | bytes 23048 | tf_op jit(solution)/shard_map/ppermute | solution.py:15
  134.2 8.3 %copy-start.4 = (bf16[1024,256]{1,0:T(8,128)(2,1)}, bf16[1024,256]{1,0:T(8,128)(2,1)S(1)}, u32[]{:S(2)}) copy-start(bf16[1024,256]{1,0:T(8,128)(2,1)S(1)} %multiply_convert_fusion.5) | copy-start | bytes 1572868
  142.5 49.8 %copy-start.14 = (f32[20]{0:T(128)S(1)}, f32[20]{0:T(128)}, u32[]{:S(2)}) copy-start(f32[20]{0:T(128)} %param.30) | copy-start | bytes 244
  142.5 51.7 %copy-start.15 = (f32[16]{0:T(128)S(1)}, f32[16]{0:T(128)}, u32[]{:S(2)}) copy-start(f32[16]{0:T(128)} %param.33) | copy-start | bytes 196
  142.5 6.7 %copy-start.6 = (bf16[4,256,128]{2,1,0:T(8,128)(2,1)}, bf16[4,256,128]{2,1,0:T(8,128)(2,1)S(1)}, u32[]{:S(2)}) copy-start(bf16[4,256,128]{2,1,0:T(8,128)(2,1)S(1)} %get-tuple-element.314) | copy-start | bytes 786436 | tf_op jit(solution)/shard_map/while
  147.5 1.7 copy-start.2
  151.1 3.6 copy-start.7
  154.7 6.7 %copy-start.6 = (bf16[4,256,128]{2,1,0:T(8,128)(2,1)}, bf16[4,256,128]{2,1,0:T(8,128)(2,1)S(1)}, u32[]{:S(2)}) copy-start(bf16[4,256,128]{2,1,0:T(8,128)(2,1)S(1)} %get-tuple-element.314) | copy-start | bytes 786436 | tf_op jit(solution)/shard_map/while
  159.7 1.7 copy-start.2
  163.2 3.6 copy-start.7
  166.9 6.7 %copy-start.6 = (bf16[4,256,128]{2,1,0:T(8,128)(2,1)}, bf16[4,256,128]{2,1,0:T(8,128)(2,1)S(1)}, u32[]{:S(2)}) copy-start(bf16[4,256,128]{2,1,0:T(8,128)(2,1)S(1)} %get-tuple-element.314) | copy-start | bytes 786436 | tf_op jit(solution)/shard_map/while
  171.8 1.7 copy-start.2
  175.4 3.7 copy-start.7
  179.1 6.7 %copy-start.6 = (bf16[4,256,128]{2,1,0:T(8,128)(2,1)}, bf16[4,256,128]{2,1,0:T(8,128)(2,1)S(1)}, u32[]{:S(2)}) copy-start(bf16[4,256,128]{2,1,0:T(8,128)(2,1)S(1)} %get-tuple-element.314) | copy-start | bytes 786436 | tf_op jit(solution)/shard_map/while
  184.0 1.7 copy-start.2
  187.6 3.6 copy-start.7
  192.0 185.6 %reduce-scatter.4.cloned.1.call-start = ((), (), s32[]{:S(2)}) async-start(), calls=%async_computation.3 | async-start | bytes 6553600
  192.3 27.5 %copy-start.5 = (bf16[1024,256]{1,0:T(8,128)(2,1)S(1)}, bf16[1024,256]{1,0:T(8,128)(2,1)}, u32[]{:S(2)}) copy-start(bf16[1024,256]{1,0:T(8,128)(2,1)} %copy-done.4) | copy-start | bytes 1572868
  230.2 27.3 %copy-start.11 = (f32[1280]{0:T(1024)S(1)}, f32[1280]{0:T(1024)}, u32[]{:S(2)}) copy-start(f32[1280]{0:T(1024)} %param.31) | copy-start | bytes 15364
  278.2 102.4 %copy-start.1 = (bf16[2560,256]{1,0:T(8,128)(2,1)S(1)}, bf16[2560,256]{1,0:T(8,128)(2,1)}, u32[]{:S(2)}) copy-start(bf16[2560,256]{1,0:T(8,128)(2,1)} %param.22) | copy-start | bytes 3932164
Sparse Core Ops, SparseCore 0:
  9.6 100.7 all-gather.4
  192.2 27.4 all-gather.6
  278.4 99.2 reduce-scatter.3
where the time goes:
time: 390 us; the launch traced here: 387 us
  waiting for transfers between devices  149 us (38%)
  blocking collectives  74.8 us (19%)
  matrix products  67.1 us (17%)
  local copies, waits for them, and re-layouts  37.9 us (10%)
  other arithmetic  36.9 us (9%)
  between operations  15.3 us (4%)
  starting transfers between devices  5.96 us (2%)
    all_gather x1, waiting for transfers between devices, shards(): piece = lax.all_gather(hidden, 'tp', axis=1, tiled=True)  100 us
    pmax x1, blocking collectives, shards(): peak_value = lax.pmax(jnp.max(jnp.abs(normed)), ('seq', 'tp'))  51 us
    unnamed x4, waiting for transfers between devices  43.9 us
    dot_general x4, matrix products, shards(): jnp.dot(piece, matrix, preferred_element_type=jnp.float32)  31.9 us
    dot_general x1, matrix products, shards(): partial_value = jnp.dot(quant, out_proj, preferred_element_type=jnp.float32)  12.8 us
    unnamed x34, local copies, waits for them, and re-layouts  12.1 us
    unnamed x1, blocking collectives  12.1 us
    psum x1, blocking collectives, shards(): squares = lax.psum(local_squares, 'tp')  11.7 us
  transfers between devices with their start and end apart: 5, of which 3 were waited for; matrix products, arithmetic and copies ran while one was open for 8% of the time, Pallas kernels for 0%

commit v1 on v0

--- a/solution.py
+++ b/solution.py
@@ -1,3 +1,4 @@
+import functools
 import jax
 import jax.numpy as jnp
 from jax import lax
@@ -7,6 +8,22 @@
 INNER = 5120
 QMAX = 448.0
 EPS = 1e-05
+
+
+def put_windows(local_x, ndim_at):
+    shares = lax.axis_size("tp")
+    lower = [(idx - 1, idx) for idx in range(1, shares)] + [(shares - 1, 0)]
+    y_new = local_x
+    entries = [y_new]
+    for _ in range(shares - 1):
+        y_new = lax.ppermute(y_new, perm=lower, axis_name="tp")
+        entries += [y_new]
+    response = jnp.concatenate([*reversed(entries)], axis=ndim_at)
+    finding = lax.axis_index("tp")
+    return jnp.roll(response, (finding + 1) * y_new.shape[ndim_at], ndim_at)
+
+
+solve_forms_up = functools.partial(put_windows, ndim_at=1)
 
 
 def shifted(x, axis, by):
@@ -99,7 +116,7 @@
     head_width = inner_local // head_count
     kernel = conv_weight.shape[0]
     matrices = (gate_proj, input_proj, bc_proj, step_proj)
-    piece = lax.all_gather(hidden, "tp", axis=1, tiled=True)
+    piece = solve_forms_up(hidden)
     gate_raw, x_raw, bc_raw, step_raw = tuple(
         (jnp.dot(piece, matrix, preferred_element_type=jnp.float32) for matrix in matrices)
     )

time: 390 us -> 390 us (level)
  local copies, waits for them, and re-layouts: 37.9 us -> 47 us
  waiting for transfers between devices: 149 us -> 140 us
    all_gather x1 -> x0, waiting for transfers between devices: 100 us -> none  [shards(): piece = lax.all_gather(hidden, 'tp', axis=1, tiled=True)]
    ppermute x0 -> x3, waiting for transfers between devices: none -> 91 us  [put_windows(): y_new = lax.ppermute(y_new, perm=lower, axis_name='tp')]
    unnamed x34 -> x51, local copies, waits for them, and re-layouts: 12.1 us -> 20.3 us
    unnamed x4 -> x3, waiting for transfers between devices: 43.9 us -> 43.2 us
  transfers between devices with their start and end apart: 5 -> 7, of which waited for: 3 -> 5; matrix products, arithmetic and copies ran while one was open for 8% -> 9% of each run, Pallas kernels for 0% -> 0%
where the time goes in v1:
time: 390 us; the launch traced here: 387 us
  waiting for transfers between devices  140 us (36%)
  blocking collectives  74.5 us (19%)
  matrix products  66.9 us (17%)
  local copies, waits for them, and re-layouts  47 us (12%)
  other arithmetic  34 us (9%)
  between operations  15.8 us (4%)
  starting transfers between devices  8.35 us (2%)
    ppermute x3, waiting for transfers between devices, put_windows(): y_new = lax.ppermute(y_new, perm=lower, axis_name='tp')  91 us
    pmax x1, blocking collectives, shards(): peak_value = lax.pmax(jnp.max(jnp.abs(normed)), ('seq', 'tp'))  51 us
    unnamed x3, waiting for transfers between devices  43.2 us
    dot_general x4, matrix products, shards(): jnp.dot(piece, matrix, preferred_element_type=jnp.float32)  31.8 us
    unnamed x51, local copies, waits for them, and re-layouts  20.3 us
    dot_general x1, matrix products, shards(): partial_value = jnp.dot(quant, out_proj, preferred_element_type=jnp.float32)  12.7 us
    unnamed x1, blocking collectives  11.9 us
    psum x1, blocking collectives, shards(): squares = lax.psum(local_squares, 'tp')  11.6 us
  transfers between devices with their start and end apart: 7, of which 5 were waited for; matrix products, arithmetic and copies ran while one was open for 9% of the time, Pallas kernels for 0%

profile of v1, /device:TPU:0, one launch (start us, length us, event | category | flops | bytes accessed | tf_op | source)
XLA Modules:
  0.0 387.2 jit_solution(15589827454237731181)
XLA Ops:
  7.2 3.1 collective-permute-start
  10.3 31.0 %collective-permute-done = bf16[1024,640]{1,0:T(8,128)(2,1)S(1)} collective-permute-done((bf16[1024,640]{1,0:T(8,128)(2,1)}, bf16[1024,640]{1,0:T(8,128)(2,1)S(1)}, u32[]{:S(2)}, u32[]{:S(2)}) %collective-permute-start) | collective-permute-done | bytes 1310752 | tf_op jit(solution)/shard_map/ppermute | solution.py:19
  42.4 31.8 %collective-permute-done.1 = bf16[1024,640]{1,0:T(8,128)(2,1)} collective-permute-done((bf16[1024,640]{1,0:T(8,128)(2,1)S(1)}, bf16[1024,640]{1,0:T(8,128)(2,1)}, u32[]{:S(2)}, u32[]{:S(2)}) %collective-permute-start.1) | collective-permute-done | bytes 1310752 | tf_op jit(solution)/shard_map/ppermute | solution.py:19
  74.3 1.5 slice_reduce_fusion.5
  77.3 28.2 %collective-permute-done.2 = bf16[1024,640]{1,0:T(8,128)(2,1)} collective-permute-done((bf16[1024,640]{1,0:T(8,128)(2,1)}, bf16[1024,640]{1,0:T(8,128)(2,1)}, u32[]{:S(2)}, u32[]{:S(2)}) %collective-permute-start.2) | collective-permute-done | bytes 1310752 | tf_op jit(solution)/shard_map/ppermute | solution.py:19
  105.5 1.5 constant_dynamic-update-slice_fusion.8
  107.0 1.6 constant_dynamic-update-slice_fusion.7
  109.1 1.6 constant_dynamic-update-slice_fusion.4
  110.7 1.6 constant_dynamic-update-slice_fusion.3
  112.9 2.2 fusion.45
  115.1 1.3 collective-permute-start.4
  116.4 2.9 fusion.54
  120.2 11.1 %convolution_convert_fusion.2 = bf16[1024,1280]{1,0:T(8,128)(2,1)S(1)} fusion(bf16[2560,1280]{1,0:T(8,128)(2,1)} %param.21, bf16[1024,5120]{1,0:T(8,128)(2,1)} %copy-done.10, s32[]{:T(128)S(6)} %select_n.35), kind=kOutput, calls=%fused_computation.58 | convolution fusion | flops 6712197120 | bytes 14417924 | tf_op jit(solution)/shard_map/dot_general | solution.py:121
  131.3 3.9 collective-permute-start.3
  136.8 4.7 %multiply_convert_fusion.4 = bf16[1024,1280]{1,0:T(8,128)(2,1)} fusion(bf16[1024,1280]{1,0:T(8,128)(2,1)S(1)} %convolution_convert_fusion.2, bf16[3,1280]{1,0:T(4,128)(2,1)S(1)} %collective-permute-done.3, f32[1280]{0:T(1024)S(1)} %copy-done.13, f32[1280]{0:T(1024)S(1)} %copy-done.11, f32[1280]{0:T(1024)S(1)} %copy-done.12, f32[1280]{0:T(1024)S(1)} %get-tuple-element.152, ...), kind=kLoop, calls=%fused_computation.56 | loop fusion | flops 34078720 | bytes 5276160 | tf_op jit(solution)/shard_map/convert_element_type | solution.py:62
  141.5 48.6 %while.26 = (s32[]{:T(128)}, f32[20,64,128]{2,1,0:T(8,128)S(1)}, f32[4,256,1280]{2,1,0:T(8,128)}, f32[4,20,256]{2,1,0:T(8,128)}, f32[4,20,256]{2,1,0:T(8,128)}, ...) while((s32[]{:T(128)}, f32[20,64,128]{2,1,0:T(8,128)S(1)}, ...), condition=%wide.region_3.4_spmd.clone, body=%wide.region_0.3_spmd.clone.sunk | while | flops 782641216 | bytes 22548344 | solution.py:144
  143.5 1.4 multiply_bitcast_fusion.2
  146.5 1.7 fusion.97
  148.2 1.4 fusion.98
  151.2 1.2 fusion.95
  155.6 1.4 multiply_bitcast_fusion.2
  158.7 1.7 fusion.97
  160.4 1.4 fusion.98
  163.4 1.2 fusion.95
  167.8 1.4 multiply_bitcast_fusion.2
  170.8 1.7 fusion.97
  172.5 1.4 fusion.98
  175.6 1.2 fusion.95
  179.9 1.4 multiply_bitcast_fusion.2
  183.0 1.7 fusion.97
  184.7 1.4 fusion.98
  187.7 1.2 fusion.95
  191.2 1.3 dynamic-slice
  194.7 11.9 %all-reduce = bf16[160]{0:T(256)(128)(2,1)S(1)} all-reduce(bf16[160]{0:T(256)(128)(2,1)S(1)} %dynamic-update-slice), channel_id=2, replica_groups=mesh['seq'=8,'tp'=4] {'seq'}, use_global_device_ids=true, to_apply=%add | all-reduce | flops 160 | bytes 640
  207.6 5.6 %reduce-window.16 = f32[20,8,128]{2,1,0:T(8,128)S(1)} reduce-window(f32[20,8,128]{2,1,0:T(8,128)S(1)} %slice.113, f32[]{:T(128)} %constant.82.clone.1), window={size=1x1x128 pad=0_0x0_0x127_0}, to_apply=%region_4.5 | reduce-window | flops 2600960 | bytes 163844 | tf_op jit(solution)/shard_map/reduce-window.2
  213.8 5.5 %all-gather.4.cloned.1.call-done = bf16[160,64,128]{2,1,0:T(8,128)(2,1)} async-done(((bf16[20,64,128]{2,1,0:T(8,128)(2,1)}), bf16[160,64,128]{2,1,0:T(8,128)(2,1)}) %all-gather.4.cloned.1.call-update) | async-done | bytes 2621456 | tf_op jit(solution)/shard_map/all_gather | solution.py:38
  219.6 4.4 %broadcast_multiply_fusion = f32[1024,20,64]{0,2,1:T(8,128)} fusion(f32[1024,20]{0,1:T(8,128)S(1)} %bitcast.147, f32[20,64,128]{2,1,0:T(8,128)S(1)} %get-tuple-element.91, bf16[1024,256]{1,0:T(8,128)(2,1)S(1)} %copy-done.7), kind=kOutput, calls=%fused_computation.75 | convolution fusion | flops 2014576640 | bytes 6258688 | tf_op jit(solution)/shard_map/tn,hpn->thp/dot_general | solution.py:150
  224.0 6.0 %copy.53 = f32[1024,1280]{1,0:T(8,128)} copy(f32[1024,1280]{0,1:T(8,128)} %bitcast.135) | data formatting | bytes 10485760 | tf_op jit(solution)/shard_map/reshape | solution.py:153
  230.0 15.6 %multiply_reduce_fusion = (f32[1024]{0:T(1024)S(1)}, f32[1024,1280]{1,0:T(8,128)}) fusion(bf16[2560,1280]{1,0:T(8,128)(2,1)} %param.20, bf16[1024,5120]{1,0:T(8,128)(2,1)} %copy-done.10, s32[]{:T(128)S(6)} %select_n.35, bf16[1024,1280]{1,0:T(8,128)(2,1)} %bitcast.138, f32[1280]{0:T(1024)S(1)} %mul.251, f32[1024,1280]{1,0:T(8,128)} %copy.53, ...), kind=kOutput, calls=%fused_computation.55 | convolution fusion | flops 6727924736 | bytes 30155780 | tf_op jit(solution)/shard_map/dot_general | solution.py:121
  245.6 11.6 %psum.7 = f32[1024]{0:T(1024)S(1)} all-reduce(f32[1024]{0:T(1024)S(1)} %get-tuple-element.195), channel_id=1, replica_groups=mesh['seq'=8,'tp'=4] {'tp'}, use_global_device_ids=true, to_apply=%region_10.11 | all-reduce | flops 1024 | bytes 8192 | tf_op jit(solution)/shard_map/psum | solution.py:160
  257.2 12.7 %convolution_convert_fusion = bf16[1024,2560]{1,0:T(8,128)(2,1)} fusion(bf16[1280,2560]{1,0:T(8,128)(2,1)} %param.32, f32[1024,1280]{1,0:T(8,128)} %get-tuple-element.196, f32[]{:T(128)S(6)} %div.31, f32[1280]{0:T(1024)S(1)} %copy-done.14, f32[1024]{0:T(1024)S(1)} %add_rsqrt_fusion), kind=kOutput, calls=%fused_computation.45 | convolution fusion | flops 6720061440 | bytes 17048580 | tf_op jit(solution)/shard_map/dot_general | solution.py:166
  270.0 8.0 %copy.54 = bf16[1024,2560]{0,1:T(8,128)(2,1)} copy(bf16[1024,2560]{1,0:T(8,128)(2,1)} %convolution_convert_fusion) | data formatting | bytes 10485760
  278.0 4.0 %abs_reduce_fusion = f32[]{:T(128)} fusion(f32[1024,1280]{1,0:T(8,128)} %get-tuple-element.196, f32[1280]{0:T(1024)S(1)} %copy-done.14, f32[1024]{0:T(1024)S(1)} %add_rsqrt_fusion), kind=kLoop, calls=%fused_computation.52 | loop fusion | flops 5242879 | bytes 5252100 | tf_op jit(solution)/shard_map/reduce_max | solution.py:163
  281.9 51.0 %pmax.7 = f32[1]{0:T(128)} all-reduce(f32[1]{0:T(128)} %bitcast.19), channel_id=1, replica_groups=mesh['seq'=8,'tp'=4] {'seq','tp'}, use_global_device_ids=true, to_apply=%region_14.15 | all-reduce | flops 1 | bytes 8 | tf_op jit(solution)/shard_map/pmax | solution.py:163
  332.9 1.2 pad_maximum_fusion.2
  334.2 43.2 %reduce-scatter.4.cloned.1.call-done = bf16[640,1024]{1,0:T(8,128)(2,1)} async-done(((bf16[2560,1024]{1,0:T(8,128)(2,1)}), bf16[640,1024]{1,0:T(8,128)(2,1)}) %reduce-scatter.4.cloned.1.call-update) | async-done | bytes 1310736
  377.4 1.7 copy.55
  379.1 1.3 divide_convert_fusion
  (184 shorter events, 34.7 us)
Async XLA Ops:
  7.2 105.7 %copy-start = (bf16[2560,256]{1,0:T(8,128)(2,1)S(1)}, bf16[2560,256]{1,0:T(8,128)(2,1)}, u32[]{:S(2)}) copy-start(bf16[2560,256]{1,0:T(8,128)(2,1)} %param.22) | copy-start | bytes 3932164
  7.2 101.7 %copy-start.3 = (bf16[1024,640]{1,0:T(8,128)(2,1)S(1)}, bf16[1024,640]{1,0:T(8,128)(2,1)}, u32[]{:S(2)}) copy-start(bf16[1024,640]{1,0:T(8,128)(2,1)} %param.19) | copy-start | bytes 3932164
  7.2 212.1 %all-gather.4.cloned.1.call-start = ((), (), s32[]{:S(2)}) async-start(), calls=%async_computation.1 | async-start | bytes 2949120 | tf_op jit(solution)/shard_map/all_gather | solution.py:38
  7.2 34.1 %collective-permute-start = (bf16[1024,640]{1,0:T(8,128)(2,1)}, bf16[1024,640]{1,0:T(8,128)(2,1)S(1)}, u32[]{:S(2)}, u32[]{:S(2)}) collective-permute-start(bf16[1024,640]{1,0:T(8,128)(2,1)} %param.19), channel_id=1, source_target_pairs={{0,1},{1,2},{2,3},{3,0},{4,5},{5,6},{6,7},{7,4},{8,9},{9,10},{10,1... | collective-permute-start | bytes 3932168 | tf_op jit(solution)/shard_map/ppermute | solution.py:19
  41.4 1.1 copy-start.4
  42.4 31.8 %collective-permute-start.1 = (bf16[1024,640]{1,0:T(8,128)(2,1)S(1)}, bf16[1024,640]{1,0:T(8,128)(2,1)}, u32[]{:S(2)}, u32[]{:S(2)}) collective-permute-start(bf16[1024,640]{1,0:T(8,128)(2,1)S(1)} %collective-permute-done), channel_id=1, source_target_pairs={{0,1},{1,2},{2,3},{3,0},{4,5},{5,6},{6,7},{7,4},{8,9},{9,10},{10,1... | collective-permute-start | bytes 3932168 | tf_op jit(solution)/shard_map/ppermute | solution.py:19
  74.3 31.2 %collective-permute-start.2 = (bf16[1024,640]{1,0:T(8,128)(2,1)}, bf16[1024,640]{1,0:T(8,128)(2,1)}, u32[]{:S(2)}, u32[]{:S(2)}) collective-permute-start(bf16[1024,640]{1,0:T(8,128)(2,1)} %collective-permute-done.1), channel_id=1, source_target_pairs={{0,1},{1,2},{2,3},{3,0},{4,5},{5,6},{6,7},{7,4},{8,9},{9,10},{10,1... | collective-permute-start | bytes 3932168 | tf_op jit(solution)/shard_map/ppermute | solution.py:19
  74.3 34.3 %copy-start.5 = (bf16[1024,640]{1,0:T(8,128)(2,1)S(1)}, bf16[1024,640]{1,0:T(8,128)(2,1)}, u32[]{:S(2)}) copy-start(bf16[1024,640]{1,0:T(8,128)(2,1)} %copy-done.4) | copy-start | bytes 3932164
  112.8 6.4 %copy-start.10 = (bf16[1024,5120]{1,0:T(8,128)(2,1)}, bf16[1024,5120]{1,0:T(8,128)(2,1)S(1)}, u32[]{:S(2)}) copy-start(bf16[1024,5120]{1,0:T(8,128)(2,1)S(1)} %constant_dynamic-update-slice_fusion.1) | copy-start | bytes 31457284
  112.8 3.5 copy-start.18
  112.9 3.5 copy-start.19
  115.1 20.9 %collective-permute-start.4 = (bf16[3,256]{1,0:T(4,128)(2,1)S(1)}, bf16[3,256]{1,0:T(4,128)(2,1)S(1)}, u32[]{:S(2)}, u32[]{:S(2)}) collective-permute-start(bf16[3,256]{1,0:T(4,128)(2,1)S(1)} %slice.104), channel_id=1, source_target_pairs={{0,4},{4,8},{8,12},{12,16},{16,20},{20,24},{24,28},{1,5},{5,9},{9,... | collective-permute-start | bytes 4616 | tf_op jit(solution)/shard_map/ppermute | solution.py:32
  120.1 15.8 %copy-start.15 = (f32[256]{0:T(256)S(1)}, f32[256]{0:T(256)}, u32[]{:S(2)}) copy-start(f32[256]{0:T(256)} %param.29) | copy-start | bytes 3076
  120.1 16.6 %copy-start.11 = (f32[1280]{0:T(1024)S(1)}, f32[1280]{0:T(1024)}, u32[]{:S(2)}) copy-start(f32[1280]{0:T(1024)} %get-tuple-element.153) | copy-start | bytes 15364
  120.2 16.6 %copy-start.12 = (f32[1280]{0:T(1024)S(1)}, f32[1280]{0:T(1024)}, u32[]{:S(2)}) copy-start(f32[1280]{0:T(1024)} %get-tuple-element.154) | copy-start | bytes 15364
  120.2 16.6 %copy-start.13 = (f32[1280]{0:T(1024)S(1)}, f32[1280]{0:T(1024)}, u32[]{:S(2)}) copy-start(f32[1280]{0:T(1024)} %param.27) | copy-start | bytes 15364
  131.3 5.4 %collective-permute-start.3 = (bf16[3,1280]{1,0:T(4,128)(2,1)S(1)}, bf16[3,1280]{1,0:T(4,128)(2,1)S(1)}, u32[]{:S(2)}, u32[]{:S(2)}) collective-permute-start(bf16[3,1280]{1,0:T(4,128)(2,1)S(1)} %slice.99), channel_id=1, source_target_pairs={{0,4},{4,8},{8,12},{12,16},{16,20},{20,24},{24,28},{1,5},{5,9},{9,... | collective-permute-start | bytes 23048 | tf_op jit(solution)/shard_map/ppermute | solution.py:32
  136.7 4.8 %copy-start.6 = (bf16[1024,256]{1,0:T(8,128)(2,1)}, bf16[1024,256]{1,0:T(8,128)(2,1)S(1)}, u32[]{:S(2)}) copy-start(bf16[1024,256]{1,0:T(8,128)(2,1)S(1)} %multiply_convert_fusion.5) | copy-start | bytes 1572868
  141.5 49.5 %copy-start.17 = (f32[20]{0:T(128)S(1)}, f32[20]{0:T(128)}, u32[]{:S(2)}) copy-start(f32[20]{0:T(128)} %param.30) | copy-start | bytes 244
  141.5 51.6 %copy-start.20 = (f32[16]{0:T(128)S(1)}, f32[16]{0:T(128)}, u32[]{:S(2)}) copy-start(f32[16]{0:T(128)} %param.33) | copy-start | bytes 196
  141.5 53.0 %copy-start.16 = (bf16[20]{0:T(256)(128)(2,1)S(1)}, bf16[20]{0:T(256)(128)(2,1)}, u32[]{:S(2)}) copy-start(bf16[20]{0:T(256)(128)(2,1)} %get-tuple-element.183) | copy-start | bytes 124
  141.5 6.7 %copy-start.8 = (bf16[4,256,128]{2,1,0:T(8,128)(2,1)}, bf16[4,256,128]{2,1,0:T(8,128)(2,1)S(1)}, u32[]{:S(2)}) copy-start(bf16[4,256,128]{2,1,0:T(8,128)(2,1)S(1)} %get-tuple-element.314) | copy-start | bytes 786436 | tf_op jit(solution)/shard_map/while
  146.5 1.7 copy-start.2
  150.0 3.6 copy-start.9
  153.7 6.7 %copy-start.8 = (bf16[4,256,128]{2,1,0:T(8,128)(2,1)}, bf16[4,256,128]{2,1,0:T(8,128)(2,1)S(1)}, u32[]{:S(2)}) copy-start(bf16[4,256,128]{2,1,0:T(8,128)(2,1)S(1)} %get-tuple-element.314) | copy-start | bytes 786436 | tf_op jit(solution)/shard_map/while
  158.6 1.7 copy-start.2
  162.2 3.6 copy-start.9
  165.9 6.7 %copy-start.8 = (bf16[4,256,128]{2,1,0:T(8,128)(2,1)}, bf16[4,256,128]{2,1,0:T(8,128)(2,1)S(1)}, u32[]{:S(2)}) copy-start(bf16[4,256,128]{2,1,0:T(8,128)(2,1)S(1)} %get-tuple-element.314) | copy-start | bytes 786436 | tf_op jit(solution)/shard_map/while
  170.8 1.7 copy-start.2
  174.4 3.6 copy-start.9
  178.0 6.7 %copy-start.8 = (bf16[4,256,128]{2,1,0:T(8,128)(2,1)}, bf16[4,256,128]{2,1,0:T(8,128)(2,1)S(1)}, u32[]{:S(2)}) copy-start(bf16[4,256,128]{2,1,0:T(8,128)(2,1)S(1)} %get-tuple-element.314) | copy-start | bytes 786436 | tf_op jit(solution)/shard_map/while
  182.9 1.7 copy-start.2
  186.5 3.6 copy-start.9
  190.9 186.4 %reduce-scatter.4.cloned.1.call-start = ((), (), s32[]{:S(2)}) async-start(), calls=%async_computation.2 | async-start | bytes 6553600
  191.0 28.6 %copy-start.7 = (bf16[1024,256]{1,0:T(8,128)(2,1)S(1)}, bf16[1024,256]{1,0:T(8,128)(2,1)}, u32[]{:S(2)}) copy-start(bf16[1024,256]{1,0:T(8,128)(2,1)} %copy-done.6) | copy-start | bytes 1572868
  230.0 27.2 %copy-start.14 = (f32[1280]{0:T(1024)S(1)}, f32[1280]{0:T(1024)}, u32[]{:S(2)}) copy-start(f32[1280]{0:T(1024)} %param.31) | copy-start | bytes 15364
  277.9 102.4 %copy-start.1 = (bf16[2560,256]{1,0:T(8,128)(2,1)S(1)}, bf16[2560,256]{1,0:T(8,128)(2,1)}, u32[]{:S(2)}) copy-start(bf16[2560,256]{1,0:T(8,128)(2,1)} %param.22) | copy-start | bytes 3932164
Sparse Core Ops, SparseCore 0:
  191.1 28.1 all-gather.3
  278.1 99.2 reduce-scatter.3
